TPU v7x, 32 devices: a whole 2x2x4 slice. The times are simulated.
32 devices in a mesh: gx: 4 (over y, core), gy: 2 (over x), gz: 4 (over z).
Axes of the slice: x: 2, y: 2, z: 4, core: 2. Of those that a mesh axis runs over, the one named last changes fastest.
Arguments:
- density: float32 [32, 32, 512], P('gx', 'gy', 'gz'), may hold values from 0.7 to 1.6
- momentum: float32 [32, 32, 512], P('gx', 'gy', 'gz'), may hold values from -7 to 7
- hydrogen: float32 [32, 32, 512], P('gx', 'gy', 'gz'), may hold values from 0.05 to 1.2
- forced_modes: int32 [96, 3], replicated, may hold values from -3 to 3, as said below
Outputs:
- density_rate: float32 [32, 32, 512], P('gx', 'gy', 'gz')
- momentum_rate: float32 [32, 32, 512], P('gx', 'gy', 'gz')
- hydrogen_rate: float32 [32, 32, 512], P('gx', 'gy', 'gz')
Inputs may be any that keep to these rules, and one draw needn't show every extreme that they name: `forced_modes`: each row is a wave vector (kx, ky, kz) with 1 <= kx^2 + ky^2 + kz^2 <= 9; the 96 rows are distinct.
All inputs are finite; a program needn't handle non-finite values.
Results may differ from a plain program's by a relative error of at most 0.0003.
Values sent between devices are 32-bit elements; how exact they have to be, the bound alone decides.
A program may use at most 64 MiB of HBM per device.

v0:
```python
import jax
import jax.numpy as jnp
from jax import lax
from jax.sharding import PartitionSpec as P

KMAX = 3
FIRST_COEFFS = (0.8, -0.2, 4.0 / 105.0, -1.0 / 280.0)
SECOND_COEFFS = (1.6, -0.2, 8.0 / 315.0, -1.0 / 560.0)
CENTRE_COEFF = -205.0 / 72.0
VISCOSITY = 0.3
DIFFUSIVITY = 1.5
FORCE_POWER = 0.3
ENERGY_EPS = 1e-06
ACTIVATION = 2.0
HIGHEST = lax.Precision.HIGHEST


def padded_2(x, sides, width):
    for axis, dim in sides:
        size, length = (lax.axis_size(axis), x.shape[dim])
        up = [(i, (i + 1) % size) for i in range(size)]
        down = [(j, i) for i, j in up]
        last = lax.slice_in_dim(x, length - width, length, axis=dim)
        first = lax.slice_in_dim(x, 0, width, axis=dim)
        before = lax.ppermute(last, axis, up)
        after = lax.ppermute(first, axis, down)
        x = jnp.concatenate([before, x, after], axis=dim)
    return x


def shifted(padded, axis, offset, length):
    return lax.slice_in_dim(padded, 4 + offset, 4 + offset + length, axis=axis)


def first_diff(padded, axis, length):
    total = jnp.zeros_like(shifted(padded, axis, 0, length))
    for offset, weight in enumerate(FIRST_COEFFS, 1):
        total = total + weight * (
            shifted(padded, axis, offset, length) - shifted(padded, axis, -offset, length)
        )
    return total


def second_diff(padded, axis, length):
    total = CENTRE_COEFF * shifted(padded, axis, 0, length)
    for offset, weight in enumerate(SECOND_COEFFS, 1):
        total = total + weight * (
            shifted(padded, axis, offset, length) + shifted(padded, axis, -offset, length)
        )
    return total


def wave_tables(start, local, total):
    position = start + jnp.arange(local, dtype=jnp.int32)
    wavenum = jnp.arange(-KMAX, KMAX + 1, dtype=jnp.int32)
    phase = wavenum[:, None] * position[None, :] % total
    angle = 2.0 * jnp.pi / total * phase.astype(jnp.float32)
    return (jnp.cos(angle), jnp.sin(angle))


def modal_force(velocity, forced_modes):
    size_x, size_y, size_z = velocity.shape
    full_x = size_x * lax.axis_size("gx")
    full_y = size_y * lax.axis_size("gy")
    full_z = size_z * lax.axis_size("gz")
    cos_x, sin_x = wave_tables(lax.axis_index("gx") * size_x, size_x, full_x)
    cos_y, sin_y = wave_tables(lax.axis_index("gy") * size_y, size_y, full_y)
    cos_z, sin_z = wave_tables(lax.axis_index("gz") * size_z, size_z, full_z)
    flat = velocity.reshape(size_x * size_y, size_z)
    contract = (((1,), (1,)), ((), ()))
    part_re = lax.dot_general(cos_z, flat, contract, precision=HIGHEST).reshape(-1, size_x, size_y)
    part_im = lax.dot_general(sin_z, flat, contract, precision=HIGHEST).reshape(-1, size_x, size_y)
    mid_re = jnp.einsum("axy,by->abx", part_re, cos_y, precision=HIGHEST) - jnp.einsum(
        "axy,by->abx", part_im, sin_y, precision=HIGHEST
    )
    mid_im = jnp.einsum("axy,by->abx", part_re, sin_y, precision=HIGHEST) + jnp.einsum(
        "axy,by->abx", part_im, cos_y, precision=HIGHEST
    )
    cube_re = jnp.einsum("abx,cx->cba", mid_re, cos_x, precision=HIGHEST) - jnp.einsum(
        "abx,cx->cba", mid_im, sin_x, precision=HIGHEST
    )
    cube_im = jnp.einsum("abx,cx->cba", mid_re, sin_x, precision=HIGHEST) + jnp.einsum(
        "abx,cx->cba", mid_im, cos_x, precision=HIGHEST
    )
    width = 2 * KMAX + 1
    code = (
        (forced_modes[:, 0] + KMAX) * width * width
        + (forced_modes[:, 1] + KMAX) * width
        + (forced_modes[:, 2] + KMAX)
    )
    selector = (code[:, None] == jnp.arange(width**3, dtype=jnp.int32)[None, :]).astype(jnp.float32)
    local_cos = jnp.dot(selector, cube_re.reshape(-1), precision=HIGHEST)
    local_sin = jnp.dot(selector, cube_im.reshape(-1), precision=HIGHEST)
    summed = lax.psum((local_cos, local_sin), ("gx", "gy", "gz"))
    ncell = float(full_x * full_y * full_z)
    coef_cos = summed[0] / ncell
    coef_sin = summed[1] / ncell
    energy = jnp.sum(coef_cos * coef_cos + coef_sin * coef_sin)
    spec_re = jnp.dot(selector.T, coef_cos, precision=HIGHEST).reshape(width, width, width)
    spec_im = -jnp.dot(selector.T, coef_sin, precision=HIGHEST).reshape(width, width, width)
    step_re = jnp.einsum("abc,ax->xbc", spec_re, cos_x, precision=HIGHEST) - jnp.einsum(
        "abc,ax->xbc", spec_im, sin_x, precision=HIGHEST
    )
    step_im = jnp.einsum("abc,ax->xbc", spec_re, sin_x, precision=HIGHEST) + jnp.einsum(
        "abc,ax->xbc", spec_im, cos_x, precision=HIGHEST
    )
    plane_re = jnp.einsum("xbc,by->xyc", step_re, cos_y, precision=HIGHEST) - jnp.einsum(
        "xbc,by->xyc", step_im, sin_y, precision=HIGHEST
    )
    plane_im = jnp.einsum("xbc,by->xyc", step_re, sin_y, precision=HIGHEST) + jnp.einsum(
        "xbc,by->xyc", step_im, cos_y, precision=HIGHEST
    )
    low = 2.0 * (
        jnp.dot(plane_re.reshape(-1, width), cos_z, precision=HIGHEST)
        - jnp.dot(plane_im.reshape(-1, width), sin_z, precision=HIGHEST)
    )
    return FORCE_POWER * low.reshape(size_x, size_y, size_z) / (energy + ENERGY_EPS)


def stencil_terms(density, momentum, hydrogen):
    size_x, size_y, size_z = density.shape
    fields = jnp.stack([density, momentum, hydrogen])
    stream_pad = padded_2(fields, (("gx", 1),), 4)
    dens_pad = stream_pad[0]
    mom_pad = stream_pad[1]
    fuel_pad = stream_pad[2]
    vel_pad = mom_pad / dens_pad
    velocity = momentum / density
    mass_div = first_diff(mom_pad, 0, size_x)
    mom_div = first_diff(mom_pad * vel_pad + dens_pad, 0, size_x)
    fuel_div = first_diff(fuel_pad * vel_pad, 0, size_x)
    diffused = second_diff(stream_pad[1:], 1, size_x)
    carried = fields[1:]
    side_pad = padded_2(carried, (("gy", 2),), 4)
    diffused = diffused + second_diff(side_pad, 2, size_y)
    depth_pad = padded_2(carried, (("gz", 3),), 4)
    diffused = diffused + second_diff(depth_pad, 3, size_z)
    density_rate = -mass_div
    momentum_part = -mom_div + VISCOSITY * diffused[0]
    hydrogen_rate = (
        -fuel_div + DIFFUSIVITY * diffused[1] - hydrogen * jnp.exp(-ACTIVATION * hydrogen / density)
    )
    return (density_rate, momentum_part, hydrogen_rate, velocity)


def per_device(density, momentum, hydrogen, forced_modes):
    density_rate, momentum_part, hydrogen_rate, velocity = stencil_terms(
        density, momentum, hydrogen
    )
    force = modal_force(velocity, forced_modes)
    momentum_rate = momentum_part + density * force
    return (density_rate, momentum_rate, hydrogen_rate)


def solution(mesh):
    in_specs = (P("gx", "gy", "gz"), P("gx", "gy", "gz"), P("gx", "gy", "gz"), P())
    out_specs = (P("gx", "gy", "gz"), P("gx", "gy", "gz"), P("gx", "gy", "gz"))
    return jax.shard_map(
        per_device, mesh=mesh, in_specs=in_specs, out_specs=out_specs, check_vma=False
    )
```

profile of v0, /device:TPU:0, one launch (start us, length us, event | category | flops | bytes accessed | tf_op | source)
XLA Modules:
  0.0 68.3 jit_solution(13561486433452275139)
XLA Ops:
  0.6 0.9 %pad_maximum_fusion.4 = f32[3,8,16,128]{3,2,1,0:T(8,128)S(1)} fusion(f32[1,8,16,128]{3,2,1,0:T(8,128)} %bitcast.128, f32[1,8,16,128]{3,2,1,0:T(8,128)} %bitcast.136, f32[1,8,16,128]{3,2,1,0:T(8,128)} %bitcast.144), kind=kLoop, calls=%fused_computation.35 | loop fusion | flops 98304 | bytes 393216 | tf_op jit(solution)/shard_map/stack | solution.py:122
  1.6 2.5 %collective-permute-start = (f32[3,4,16,128]{3,2,1,0:T(8,128)S(1)}, f32[3,4,16,128]{3,2,1,0:T(8,128)S(1)}, u32[]{:S(2)}, u32[]{:S(2)}) collective-permute-start(f32[3,4,16,128]{3,2,1,0:T(8,128)S(1)} %get-tuple-element.9), channel_id=1, source_target_pairs={{8,0},{16,8},{24,16},{0,24},{9,1},{17,9},{25,17},{1,25},{10,2},{18... | collective-permute-start | bytes 294920 | tf_op jit(solution)/shard_map/ppermute | solution.py:26
  4.1 0.1 fusion.8
  4.2 3.7 %collective-permute-start.4 = (f32[2,8,16,4]{3,2,1,0:T(8,128)S(1)}, f32[2,8,16,4]{3,2,1,0:T(8,128)S(1)}, u32[]{:S(2)}, u32[]{:S(2)}) collective-permute-start(f32[2,8,16,4]{3,2,1,0:T(8,128)S(1)} %get-tuple-element.17), channel_id=1, source_target_pairs={{1,0},{2,1},{3,2},{0,3},{5,4},{6,5},{7,6},{4,7},{9,8},{10,9},{11,1... | collective-permute-start | bytes 12296 | tf_op jit(solution)/shard_map/ppermute | solution.py:26
  7.9 1.6 %collective-permute-start.2 = (f32[2,8,4,128]{3,2,1,0:T(4,128)S(1)}, f32[2,8,4,128]{3,2,1,0:T(4,128)S(1)}, u32[]{:S(2)}, u32[]{:S(2)}) collective-permute-start(f32[2,8,4,128]{3,2,1,0:T(4,128)S(1)} %get-tuple-element.13), channel_id=1, source_target_pairs={{4,0},{0,4},{5,1},{1,5},{6,2},{2,6},{7,3},{3,7},{12,8},{8,12},{13,... | collective-permute-start | bytes 98312 | tf_op jit(solution)/shard_map/ppermute | solution.py:26
  9.4 0.6 fusion.109
  10.1 0.7 fusion.102
  10.7 0.5 fusion.86
  11.3 0.5 fusion.84
  11.8 0.5 fusion.7
  12.3 0.6 fusion.97
  12.9 0.6 fusion.112
  13.5 0.6 fusion.6
  14.1 0.6 fusion.4
  14.7 0.2 copy.29
  14.8 0.1 reshape.97
  15.0 0.6 copy-done.3
  15.5 0.6 fusion.5
  16.1 0.2 copy.25
  16.3 0.1 reshape.90
  16.4 0.2 convolution_bitcast_fusion
  16.6 0.3 convolution_bitcast_fusion.1
  16.9 39.2 %all-reduce = (f32[96]{0:T(128)S(1)}, f32[96]{0:T(128)S(1)}) all-reduce(f32[96]{0:T(128)S(1)} %convolution_bitcast_fusion.1, f32[96]{0:T(128)S(1)} %convolution_bitcast_fusion), channel_id=1, replica_groups=mesh['gx'=4,'gy'=2,'gz'=4] {'gx','gy','gz'}, use_global_device_ids=true, to_apply=%region_0.1 | all-reduce | flops 192 | bytes 1536 | tf_op jit(solution)/shard_map/psum | solution.py:94
  56.0 0.2 convolution_reduce_fusion.1
  56.3 0.1 reshape.78
  56.4 0.3 fusion.80
  56.7 0.3 fusion.78
  57.0 0.2 convolution_reduce_fusion
  57.2 0.1 neg.18
  57.3 0.3 convolution_subtract_fusion.2
  57.6 0.1 copy.31
  57.8 0.3 fusion.117
  58.1 0.3 fusion.104
  58.4 0.6 add_reduce_fusion
  59.0 0.3 convolution_add_fusion.1
  59.3 0.1 copy.34
  59.4 0.3 fusion.3
  59.7 0.1 reshape.80
  59.8 0.3 fusion.123
  60.1 0.3 fusion.2
  61.1 0.3 fusion.1
  61.5 2.3 %collective-permute-start.3 = (f32[2,8,4,128]{3,2,1,0:T(4,128)S(1)}, f32[2,8,4,128]{3,2,1,0:T(4,128)S(1)}, u32[]{:S(2)}, u32[]{:S(2)}) collective-permute-start(f32[2,8,4,128]{3,2,1,0:T(4,128)S(1)} %get-tuple-element.14), channel_id=1, source_target_pairs={{0,4},{4,0},{1,5},{5,1},{2,6},{6,2},{3,7},{7,3},{8,12},{12,8},{9,1... | collective-permute-start | bytes 98312 | tf_op jit(solution)/shard_map/ppermute | solution.py:25
  63.8 0.1 pad_maximum_fusion.2
  64.0 1.7 %collective-permute-done.3 = f32[2,8,4,128]{3,2,1,0:T(4,128)S(1)} collective-permute-done((f32[2,8,4,128]{3,2,1,0:T(4,128)S(1)}, f32[2,8,4,128]{3,2,1,0:T(4,128)S(1)}, u32[]{:S(2)}, u32[]{:S(2)}) %collective-permute-start.3) | collective-permute-done | bytes 32800 | tf_op jit(solution)/shard_map/ppermute | solution.py:25
  65.9 0.7 fusion.68
  66.6 0.3 fusion.14
  66.9 0.7 %fusion.45 = f32[8,16,128]{2,1,0:T(8,128)} fusion(f32[2,8,16,128]{3,2,1,0:T(8,128)S(1)} %fusion.14, f32[16,16,128]{2,1,0:T(8,128)S(1)} %get-tuple-element.5, f32[8,16,128]{2,1,0:T(8,128)S(1)} %copy-done, f32[8,16,128]{2,1,0:T(8,128)S(1)} %copy-done.2), kind=kLoop, calls=%fused_computation.94 | loop fusion | flops 294912 | bytes 786432 | tf_op jit(solution)/shard_map/sub | solution.py:141
  67.6 0.7 fusion.56
  (27 shorter events, 0.3 us)
Async XLA Ops:
  1.6 2.5 %copy-start = (f32[8,16,128]{2,1,0:T(8,128)S(1)}, f32[8,16,128]{2,1,0:T(8,128)}, u32[]{:S(2)}) copy-start(f32[8,16,128]{2,1,0:T(8,128)} %param.6) | copy-start | bytes 196612
  1.6 2.5 %copy-start.1 = (f32[8,16,128]{2,1,0:T(8,128)S(1)}, f32[8,16,128]{2,1,0:T(8,128)}, u32[]{:S(2)}) copy-start(f32[8,16,128]{2,1,0:T(8,128)} %param.5) | copy-start | bytes 196612
  1.6 64.2 %collective-permute-start = (f32[3,4,16,128]{3,2,1,0:T(8,128)S(1)}, f32[3,4,16,128]{3,2,1,0:T(8,128)S(1)}, u32[]{:S(2)}, u32[]{:S(2)}) collective-permute-start(f32[3,4,16,128]{3,2,1,0:T(8,128)S(1)} %get-tuple-element.9), channel_id=1, source_target_pairs={{8,0},{16,8},{24,16},{0,24},{9,1},{17,9},{25,17},{1,25},{10,2},{18... | collective-permute-start | bytes 294920 | tf_op jit(solution)/shard_map/ppermute | solution.py:26
  4.1 61.7 %collective-permute-start.1 = (f32[3,4,16,128]{3,2,1,0:T(8,128)S(1)}, f32[3,4,16,128]{3,2,1,0:T(8,128)S(1)}, u32[]{:S(2)}, u32[]{:S(2)}) collective-permute-start(f32[3,4,16,128]{3,2,1,0:T(8,128)S(1)} %get-tuple-element.10), channel_id=1, source_target_pairs={{0,8},{8,16},{16,24},{24,0},{1,9},{9,17},{17,25},{25,1},{2,10},{10... | collective-permute-start | bytes 294920 | tf_op jit(solution)/shard_map/ppermute | solution.py:25
  4.2 57.3 %collective-permute-start.4 = (f32[2,8,16,4]{3,2,1,0:T(8,128)S(1)}, f32[2,8,16,4]{3,2,1,0:T(8,128)S(1)}, u32[]{:S(2)}, u32[]{:S(2)}) collective-permute-start(f32[2,8,16,4]{3,2,1,0:T(8,128)S(1)} %get-tuple-element.17), channel_id=1, source_target_pairs={{1,0},{2,1},{3,2},{0,3},{5,4},{6,5},{7,6},{4,7},{9,8},{10,9},{11,1... | collective-permute-start | bytes 12296 | tf_op jit(solution)/shard_map/ppermute | solution.py:26
  7.9 1.6 %copy-start.2 = (f32[8,16,128]{2,1,0:T(8,128)S(1)}, f32[8,16,128]{2,1,0:T(8,128)}, u32[]{:S(2)}) copy-start(f32[8,16,128]{2,1,0:T(8,128)} %param.4) | copy-start | bytes 196612
  7.9 56.0 %collective-permute-start.5 = (f32[2,8,16,4]{3,2,1,0:T(8,128)S(1)}, f32[2,8,16,4]{3,2,1,0:T(8,128)S(1)}, u32[]{:S(2)}, u32[]{:S(2)}) collective-permute-start(f32[2,8,16,4]{3,2,1,0:T(8,128)S(1)} %get-tuple-element.18), channel_id=1, source_target_pairs={{0,1},{1,2},{2,3},{3,0},{4,5},{5,6},{6,7},{7,4},{8,9},{9,10},{10,1... | collective-permute-start | bytes 12296 | tf_op jit(solution)/shard_map/ppermute | solution.py:25
  7.9 56.1 %collective-permute-start.2 = (f32[2,8,4,128]{3,2,1,0:T(4,128)S(1)}, f32[2,8,4,128]{3,2,1,0:T(4,128)S(1)}, u32[]{:S(2)}, u32[]{:S(2)}) collective-permute-start(f32[2,8,4,128]{3,2,1,0:T(4,128)S(1)} %get-tuple-element.13), channel_id=1, source_target_pairs={{4,0},{0,4},{5,1},{1,5},{6,2},{2,6},{7,3},{3,7},{12,8},{8,12},{13,... | collective-permute-start | bytes 98312 | tf_op jit(solution)/shard_map/ppermute | solution.py:26
  14.8 0.7 %copy-start.3 = (s32[96,3]{0,1:T(4,128)S(1)}, s32[96,3]{0,1:T(4,128)}, u32[]{:S(2)}) copy-start(s32[96,3]{0,1:T(4,128)} %param.7) | copy-start | bytes 3460
  61.5 4.2 %collective-permute-start.3 = (f32[2,8,4,128]{3,2,1,0:T(4,128)S(1)}, f32[2,8,4,128]{3,2,1,0:T(4,128)S(1)}, u32[]{:S(2)}, u32[]{:S(2)}) collective-permute-start(f32[2,8,4,128]{3,2,1,0:T(4,128)S(1)} %get-tuple-element.14), channel_id=1, source_target_pairs={{0,4},{4,0},{1,5},{5,1},{2,6},{6,2},{3,7},{7,3},{8,12},{12,8},{9,1... | collective-permute-start | bytes 98312 | tf_op jit(solution)/shard_map/ppermute | solution.py:25
where the time goes:
time: 68.6 us; the launch traced here: 68.3 us
  blocking collectives  39.2 us (57%)
  starting transfers between devices  10.1 us (15%)
  matrix products  9.66 us (14%)
  other arithmetic  4.3 us (6%)
  local copies, waits for them, and re-layouts  1.83 us (3%)
  waiting for transfers between devices  1.76 us (3%)
  between operations  1.52 us (2%)
    psum x1, blocking collectives, modal_force(): summed = lax.psum((local_cos, local_sin), ('gx', 'gy', 'gz'))  39.2 us
    ppermute x3, starting transfers between devices, padded_2(): after = lax.ppermute(first, axis, down)  7.7 us
    ppermute x3, starting transfers between devices, padded_2(): before = lax.ppermute(last, axis, up)  2.35 us
    ppermute x3, waiting for transfers between devices, padded_2(): before = lax.ppermute(last, axis, up)  1.75 us
  transfers between devices with their start and end apart: 6, of which 1 were waited for; matrix products, arithmetic and copies ran while one was open for 17% of the time, Pallas kernels for 0%

commit v1 on v0

--- a/solution.py
+++ b/solution.py
@@ -91,7 +91,7 @@
     selector = (code[:, None] == jnp.arange(width**3, dtype=jnp.int32)[None, :]).astype(jnp.float32)
     local_cos = jnp.dot(selector, cube_re.reshape(-1), precision=HIGHEST)
     local_sin = jnp.dot(selector, cube_im.reshape(-1), precision=HIGHEST)
-    summed = lax.psum((local_cos, local_sin), ("gx", "gy", "gz"))
+    summed = lax.psum(lax.psum((local_cos, local_sin), "gx"), ("gy", "gz"))
     ncell = float(full_x * full_y * full_z)
     coef_cos = summed[0] / ncell
     coef_sin = summed[1] / ncell

time: 68.6 us -> 56.9 us (0.83)
  blocking collectives: 39.2 us -> 27.7 us
  starting transfers between devices: 10.1 us -> 9.26 us
    psum x1 -> x2, blocking collectives: 39.2 us -> 27.7 us  [modal_force(): summed = lax.psum(lax.psum((local_cos, local_sin), 'gx'), ('gy', 'gz'))]
    ppermute x3, starting transfers between devices: 2.35 us -> 1.56 us  [padded_2(): before = lax.ppermute(last, axis, up)]
  transfers between devices with their start and end apart: 6 -> 6, of which waited for: 1 -> 1; matrix products, arithmetic and copies ran while one was open for 17% -> 21% of each run, Pallas kernels for 0% -> 0%
where the time goes in v1:
time: 56.9 us; the launch traced here: 56.6 us
  blocking collectives  27.7 us (49%)
  matrix products  9.67 us (17%)
  starting transfers between devices  9.26 us (16%)
  other arithmetic  4.3 us (8%)
  waiting for transfers between devices  2.29 us (4%)
  local copies, waits for them, and re-layouts  1.82 us (3%)
  between operations  1.53 us (3%)
    psum x2, blocking collectives, modal_force(): summed = lax.psum(lax.psum((local_cos, local_sin), 'gx'), ('gy', 'gz'))  27.7 us
    ppermute x3, starting transfers between devices, padded_2(): after = lax.ppermute(first, axis, down)  7.7 us
    ppermute x3, waiting for transfers between devices, padded_2(): before = lax.ppermute(last, axis, up)  2.28 us
    ppermute x3, starting transfers between devices, padded_2(): before = lax.ppermute(last, axis, up)  1.56 us
  transfers between devices with their start and end apart: 6, of which 1 were waited for; matrix products, arithmetic and copies ran while one was open for 21% of the time, Pallas kernels for 0%

profile of v1, /device:TPU:0, one launch (start us, length us, event | category | flops | bytes accessed | tf_op | source)
XLA Modules:
  0.0 56.6 jit_solution(10331776919333260888)
XLA Ops:
  0.6 0.9 %pad_maximum_fusion.4 = f32[3,8,16,128]{3,2,1,0:T(8,128)S(1)} fusion(f32[1,8,16,128]{3,2,1,0:T(8,128)} %bitcast.128, f32[1,8,16,128]{3,2,1,0:T(8,128)} %bitcast.136, f32[1,8,16,128]{3,2,1,0:T(8,128)} %bitcast.144), kind=kLoop, calls=%fused_computation.35 | loop fusion | flops 98304 | bytes 393216 | tf_op jit(solution)/shard_map/stack | solution.py:122
  1.6 2.5 %collective-permute-start = (f32[3,4,16,128]{3,2,1,0:T(8,128)S(1)}, f32[3,4,16,128]{3,2,1,0:T(8,128)S(1)}, u32[]{:S(2)}, u32[]{:S(2)}) collective-permute-start(f32[3,4,16,128]{3,2,1,0:T(8,128)S(1)} %get-tuple-element.11), channel_id=1, source_target_pairs={{8,0},{16,8},{24,16},{0,24},{9,1},{17,9},{25,17},{1,25},{10,2},{18... | collective-permute-start | bytes 294920 | tf_op jit(solution)/shard_map/ppermute | solution.py:26
  4.1 0.1 fusion.8
  4.2 3.7 %collective-permute-start.4 = (f32[2,8,16,4]{3,2,1,0:T(8,128)S(1)}, f32[2,8,16,4]{3,2,1,0:T(8,128)S(1)}, u32[]{:S(2)}, u32[]{:S(2)}) collective-permute-start(f32[2,8,16,4]{3,2,1,0:T(8,128)S(1)} %get-tuple-element.19), channel_id=1, source_target_pairs={{1,0},{2,1},{3,2},{0,3},{5,4},{6,5},{7,6},{4,7},{9,8},{10,9},{11,1... | collective-permute-start | bytes 12296 | tf_op jit(solution)/shard_map/ppermute | solution.py:26
  7.9 1.6 %collective-permute-start.2 = (f32[2,8,4,128]{3,2,1,0:T(4,128)S(1)}, f32[2,8,4,128]{3,2,1,0:T(4,128)S(1)}, u32[]{:S(2)}, u32[]{:S(2)}) collective-permute-start(f32[2,8,4,128]{3,2,1,0:T(4,128)S(1)} %get-tuple-element.15), channel_id=1, source_target_pairs={{4,0},{0,4},{5,1},{1,5},{6,2},{2,6},{7,3},{3,7},{12,8},{8,12},{13,... | collective-permute-start | bytes 98312 | tf_op jit(solution)/shard_map/ppermute | solution.py:26
  9.4 0.6 %fusion.109 = f32[7,8,16]{2,0,1:T(8,128)S(1)} fusion(s32[128]{0:T(128)S(1)} %iota_add_fusion, s32[7]{0:T(128)S(1)} %iota_add_fusion.3, f32[8,16,128]{2,1,0:T(8,128)S(1)} %copy-done.1, f32[8,16,128]{2,1,0:T(8,128)S(1)} %copy-done.2), kind=kOutput, calls=%fused_computation.186 | convolution fusion | flops 1405184 | bytes 135196 | tf_op jit(solution)/shard_map/dot_general | solution.py:71
  10.1 0.7 %fusion.102 = f32[7,8,16]{2,0,1:T(8,128)S(1)} fusion(s32[128]{0:T(128)S(1)} %iota_add_fusion, s32[7]{0:T(128)S(1)} %iota_add_fusion.3, f32[8,16,128]{2,1,0:T(8,128)S(1)} %copy-done.1, f32[8,16,128]{2,1,0:T(8,128)S(1)} %copy-done.2), kind=kOutput, calls=%fused_computation.179 | convolution fusion | flops 1405184 | bytes 135196 | tf_op jit(solution)/shard_map/dot_general | solution.py:72
  10.7 0.5 fusion.86
  11.3 0.5 fusion.84
  11.8 0.5 fusion.7
  12.3 0.6 %fusion.97 = f32[7,7,7]{2,0,1:T(8,128)S(1)} fusion(f32[7,7,8]{2,1,0:T(8,128)S(1)} %fusion.7, s32[8]{0:T(128)S(1)} %iota_add_fusion.1, s32[7]{0:T(128)S(1)} %iota_add_fusion.3), kind=kOutput, calls=%fused_computation.174 | convolution fusion | flops 33712 | bytes 3000 | tf_op jit(solution)/shard_map/abx,cx->cba/dot_general | solution.py:82
  12.9 0.6 %fusion.112 = f32[7,7,7]{2,0,1:T(8,128)S(1)} fusion(f32[7,7,8]{2,1,0:T(8,128)S(1)} %fusion.7, s32[8]{0:T(128)S(1)} %iota_add_fusion.1, s32[7]{0:T(128)S(1)} %iota_add_fusion.3), kind=kOutput, calls=%fused_computation.189 | convolution fusion | flops 33712 | bytes 3000 | tf_op jit(solution)/shard_map/abx,cx->cba/dot_general | solution.py:79
  13.5 0.6 fusion.6
  14.1 0.6 %fusion.4 = f32[7,7,7]{1,0,2:T(8,128)S(1)} fusion(f32[7,7,7]{2,0,1:T(8,128)S(1)} %fusion.97, f32[7,7,8]{2,1,0:T(8,128)S(1)} %fusion.6, s32[8]{0:T(128)S(1)} %iota_add_fusion.1, s32[7]{0:T(128)S(1)} %iota_add_fusion.3), kind=kOutput, calls=%fused_computation.10 | convolution fusion | flops 34055 | bytes 4372 | tf_op jit(solution)/shard_map/abx,cx->cba/dot_general | solution.py:82
  14.7 0.2 copy.29
  14.8 0.1 reshape.97
  15.0 0.6 copy-done.3
  15.5 0.6 %fusion.5 = f32[7,7,7]{1,0,2:T(8,128)S(1)} fusion(f32[7,7,7]{2,0,1:T(8,128)S(1)} %fusion.112, f32[7,7,8]{2,1,0:T(8,128)S(1)} %fusion.6, s32[8]{0:T(128)S(1)} %iota_add_fusion.1, s32[7]{0:T(128)S(1)} %iota_add_fusion.3), kind=kOutput, calls=%fused_computation.12 | convolution fusion | flops 34055 | bytes 4372 | tf_op jit(solution)/shard_map/abx,cx->cba/dot_general | solution.py:79
  16.1 0.2 copy.25
  16.3 0.1 reshape.90
  16.4 0.2 convolution_bitcast_fusion
  16.6 0.3 convolution_bitcast_fusion.1
  16.9 6.9 %all-reduce.1 = (f32[96]{0:T(128)S(1)}, f32[96]{0:T(128)S(1)}) all-reduce(f32[96]{0:T(128)S(1)} %convolution_bitcast_fusion.1, f32[96]{0:T(128)S(1)} %convolution_bitcast_fusion), channel_id=1, replica_groups=mesh['gx'=4,'gy'=2,'gz'=4] {'gx'}, use_global_device_ids=true, to_apply=%region_0.1 | all-reduce | flops 192 | bytes 1536 | tf_op jit(solution)/shard_map/psum | solution.py:94
  23.8 20.8 %all-reduce = (f32[96]{0:T(128)S(1)}, f32[96]{0:T(128)S(1)}) all-reduce(f32[96]{0:T(128)S(1)} %get-tuple-element.5, f32[96]{0:T(128)S(1)} %get-tuple-element.6), channel_id=1, replica_groups=mesh['gx'=4,'gy'=2,'gz'=4] {'gy','gz'}, use_global_device_ids=true, to_apply=%region_1.2 | all-reduce | flops 192 | bytes 1536 | tf_op jit(solution)/shard_map/psum | solution.py:94
  44.6 0.2 convolution_reduce_fusion.1
  44.8 0.1 reshape.78
  45.0 0.3 fusion.80
  45.2 0.3 fusion.78
  45.5 0.2 convolution_reduce_fusion
  45.8 0.1 neg.18
  45.9 0.3 convolution_subtract_fusion.2
  46.2 0.1 copy.31
  46.3 0.3 fusion.104
  46.6 0.3 fusion.117
  46.9 0.6 %add_reduce_fusion = f32[]{:T(128)} fusion(f32[96]{0:T(128)S(1)} %get-tuple-element.4, f32[96]{0:T(128)S(1)} %get-tuple-element.3), kind=kLoop, calls=%fused_computation.207 | loop fusion | flops 575 | bytes 772 | tf_op jit(solution)/shard_map/reduce_sum | solution.py:98
  47.5 0.3 convolution_add_fusion.1
  47.8 0.1 copy.34
  48.0 0.3 fusion.2
  48.3 0.3 fusion.3
  48.7 0.3 fusion.123
  49.7 0.3 fusion.1
  50.0 1.6 %collective-permute-start.3 = (f32[2,8,4,128]{3,2,1,0:T(4,128)S(1)}, f32[2,8,4,128]{3,2,1,0:T(4,128)S(1)}, u32[]{:S(2)}, u32[]{:S(2)}) collective-permute-start(f32[2,8,4,128]{3,2,1,0:T(4,128)S(1)} %get-tuple-element.16), channel_id=1, source_target_pairs={{0,4},{4,0},{1,5},{5,1},{2,6},{6,2},{3,7},{7,3},{8,12},{12,8},{9,1... | collective-permute-start | bytes 98312 | tf_op jit(solution)/shard_map/ppermute | solution.py:25
  51.6 0.1 pad_maximum_fusion.2
  51.8 2.3 %collective-permute-done.3 = f32[2,8,4,128]{3,2,1,0:T(4,128)S(1)} collective-permute-done((f32[2,8,4,128]{3,2,1,0:T(4,128)S(1)}, f32[2,8,4,128]{3,2,1,0:T(4,128)S(1)}, u32[]{:S(2)}, u32[]{:S(2)}) %collective-permute-start.3) | collective-permute-done | bytes 32800 | tf_op jit(solution)/shard_map/ppermute | solution.py:25
  54.2 0.7 %fusion.68 = f32[8,16,128]{2,1,0:T(8,128)} fusion(f32[3,12,16,128]{3,2,1,0:T(8,128)S(1)} %get-tuple-element.10, f32[3,12,16,128]{3,2,1,0:T(8,128)S(1)} %get-tuple-element.9), kind=kLoop, calls=%fused_computation.127 | loop fusion | flops 196608 | bytes 589824 | tf_op jit(solution)/shard_map/neg | solution.py:138
  54.9 0.3 fusion.14
  55.2 0.7 %fusion.45 = f32[8,16,128]{2,1,0:T(8,128)} fusion(f32[2,8,16,128]{3,2,1,0:T(8,128)S(1)} %fusion.14, f32[16,16,128]{2,1,0:T(8,128)S(1)} %get-tuple-element.7, f32[8,16,128]{2,1,0:T(8,128)S(1)} %copy-done, f32[8,16,128]{2,1,0:T(8,128)S(1)} %copy-done.2), kind=kLoop, calls=%fused_computation.94 | loop fusion | flops 294912 | bytes 786432 | tf_op jit(solution)/shard_map/sub | solution.py:141
  55.9 0.7 %fusion.56 = f32[8,16,128]{2,1,0:T(8,128)} fusion(f32[2,8,16,128]{3,2,1,0:T(8,128)S(1)} %fusion.14, f32[16,16,128]{2,1,0:T(8,128)S(1)} %get-tuple-element.8, f32[8,16,128]{2,1,0:T(8,128)S(1)} %copy-done.2, f32[8,16,128]{2,1,0:T(8,128)S(1)} %bitcast.147), kind=kLoop, calls=%fused_computation.110 | loop fusion | flops 262144 | bytes 786432 | tf_op jit(solution)/shard_map/add | solution.py:151
  (28 shorter events, 0.4 us)
Async XLA Ops:
  1.6 2.5 %copy-start = (f32[8,16,128]{2,1,0:T(8,128)S(1)}, f32[8,16,128]{2,1,0:T(8,128)}, u32[]{:S(2)}) copy-start(f32[8,16,128]{2,1,0:T(8,128)} %param.6) | copy-start | bytes 196612
  1.6 2.5 %copy-start.1 = (f32[8,16,128]{2,1,0:T(8,128)S(1)}, f32[8,16,128]{2,1,0:T(8,128)}, u32[]{:S(2)}) copy-start(f32[8,16,128]{2,1,0:T(8,128)} %param.5) | copy-start | bytes 196612
  1.6 52.5 %collective-permute-start = (f32[3,4,16,128]{3,2,1,0:T(8,128)S(1)}, f32[3,4,16,128]{3,2,1,0:T(8,128)S(1)}, u32[]{:S(2)}, u32[]{:S(2)}) collective-permute-start(f32[3,4,16,128]{3,2,1,0:T(8,128)S(1)} %get-tuple-element.11), channel_id=1, source_target_pairs={{8,0},{16,8},{24,16},{0,24},{9,1},{17,9},{25,17},{1,25},{10,2},{18... | collective-permute-start | bytes 294920 | tf_op jit(solution)/shard_map/ppermute | solution.py:26
  4.1 50.0 %collective-permute-start.1 = (f32[3,4,16,128]{3,2,1,0:T(8,128)S(1)}, f32[3,4,16,128]{3,2,1,0:T(8,128)S(1)}, u32[]{:S(2)}, u32[]{:S(2)}) collective-permute-start(f32[3,4,16,128]{3,2,1,0:T(8,128)S(1)} %get-tuple-element.12), channel_id=1, source_target_pairs={{0,8},{8,16},{16,24},{24,0},{1,9},{9,17},{17,25},{25,1},{2,10},{10... | collective-permute-start | bytes 294920 | tf_op jit(solution)/shard_map/ppermute | solution.py:25
  4.2 45.8 %collective-permute-start.4 = (f32[2,8,16,4]{3,2,1,0:T(8,128)S(1)}, f32[2,8,16,4]{3,2,1,0:T(8,128)S(1)}, u32[]{:S(2)}, u32[]{:S(2)}) collective-permute-start(f32[2,8,16,4]{3,2,1,0:T(8,128)S(1)} %get-tuple-element.19), channel_id=1, source_target_pairs={{1,0},{2,1},{3,2},{0,3},{5,4},{6,5},{7,6},{4,7},{9,8},{10,9},{11,1... | collective-permute-start | bytes 12296 | tf_op jit(solution)/shard_map/ppermute | solution.py:26
  7.9 1.6 %copy-start.2 = (f32[8,16,128]{2,1,0:T(8,128)S(1)}, f32[8,16,128]{2,1,0:T(8,128)}, u32[]{:S(2)}) copy-start(f32[8,16,128]{2,1,0:T(8,128)} %param.4) | copy-start | bytes 196612
  7.9 43.8 %collective-permute-start.5 = (f32[2,8,16,4]{3,2,1,0:T(8,128)S(1)}, f32[2,8,16,4]{3,2,1,0:T(8,128)S(1)}, u32[]{:S(2)}, u32[]{:S(2)}) collective-permute-start(f32[2,8,16,4]{3,2,1,0:T(8,128)S(1)} %get-tuple-element.20), channel_id=1, source_target_pairs={{0,1},{1,2},{2,3},{3,0},{4,5},{5,6},{6,7},{7,4},{8,9},{9,10},{10,1... | collective-permute-start | bytes 12296 | tf_op jit(solution)/shard_map/ppermute | solution.py:25
  7.9 43.9 %collective-permute-start.2 = (f32[2,8,4,128]{3,2,1,0:T(4,128)S(1)}, f32[2,8,4,128]{3,2,1,0:T(4,128)S(1)}, u32[]{:S(2)}, u32[]{:S(2)}) collective-permute-start(f32[2,8,4,128]{3,2,1,0:T(4,128)S(1)} %get-tuple-element.15), channel_id=1, source_target_pairs={{4,0},{0,4},{5,1},{1,5},{6,2},{2,6},{7,3},{3,7},{12,8},{8,12},{13,... | collective-permute-start | bytes 98312 | tf_op jit(solution)/shard_map/ppermute | solution.py:26
  14.8 0.7 %copy-start.3 = (s32[96,3]{0,1:T(4,128)S(1)}, s32[96,3]{0,1:T(4,128)}, u32[]{:S(2)}) copy-start(s32[96,3]{0,1:T(4,128)} %param.7) | copy-start | bytes 3460
  50.0 4.0 %collective-permute-start.3 = (f32[2,8,4,128]{3,2,1,0:T(4,128)S(1)}, f32[2,8,4,128]{3,2,1,0:T(4,128)S(1)}, u32[]{:S(2)}, u32[]{:S(2)}) collective-permute-start(f32[2,8,4,128]{3,2,1,0:T(4,128)S(1)} %get-tuple-element.16), channel_id=1, source_target_pairs={{0,4},{4,0},{1,5},{5,1},{2,6},{6,2},{3,7},{7,3},{8,12},{12,8},{9,1... | collective-permute-start | bytes 98312 | tf_op jit(solution)/shard_map/ppermute | solution.py:25
